TPU v7x, 1024 devices: a whole 4x4x32 slice. The times are simulated.
1024 devices in a mesh: dp: 16 (over x_lo, y, core), tensor: 64 (over x_hi, z).
Axes of the slice: x: 4 (x_hi: 2, x_lo: 2; x = x_hi * 2 + x_lo), y: 4, z: 32, core: 2. Of those that a mesh axis runs over, the one named last changes fastest.
Arguments:
- query_latent: bfloat16 [2048, 1536], P(('dp', 'tensor')), may hold values from -40 to 40
- key_value_latent: bfloat16 [2048, 512], P(('dp', 'tensor')), may hold values from -40 to 40
- query_gain: float32 [1536], replicated, may hold values from 0.5 to 1.5
- key_value_gain: float32 [512], replicated, may hold values from 0.5 to 1.5
- q_up: bfloat16 [1536, 24576], P(None, 'tensor'), may hold values from -0.625 to 0.625
- kv_up: bfloat16 [512, 32768], P(None, 'tensor'), may hold values from -1 to 1
- grad_q: bfloat16 [2048, 24576], P('dp', 'tensor'), may hold values from -0.23925781 to 0.23925781
- grad_kv: bfloat16 [2048, 32768], P('dp', 'tensor'), may hold values from -0.23925781 to 0.23925781
Outputs:
- query_latent_gradient: float32 [2048, 1536], P(('dp', 'tensor'))
- key_value_latent_gradient: float32 [2048, 512], P(('dp', 'tensor'))
- d_q_up: float32 [1536, 24576], P('dp', 'tensor')
- d_kv_up: float32 [512, 32768], P('dp', 'tensor')
All inputs are finite; a program needn't handle non-finite values.
Results may differ from a plain program's by a relative error of at most 0.0029.
Values may be sent and summed in bfloat16 or wider, within the bound.
A program may use at most 32 MiB of HBM per device.

v0:
```python
import jax
import jax.numpy as jnp
from jax import lax
from jax.sharding import Mesh
from jax.sharding import PartitionSpec as P

TENSOR = ("tensor_0", "tensor_1")
DP_TENSOR = ("dp", "tensor_0", "tensor_1")


EPS = 1e-06


def in_order(pieces, dim):
    lengths = list(pieces.shape[1:])
    lengths[dim] *= pieces.shape[0]
    return jnp.moveaxis(pieces, 0, dim).reshape(lengths)


def one_gather(arrays, axis, dims):
    line = jnp.concatenate([a.reshape(-1) for a in arrays])
    lines, at, outs = (lax.all_gather(line, axis), 0, [])
    for a, dim in zip(arrays, dims):
        pieces = lines[:, at : at + a.size].reshape(-1, *a.shape)
        outs.append(in_order(pieces, dim))
        at += a.size
    return tuple(outs)


def split_up(array, dim, devices):
    lengths = array.shape
    pieces = array.reshape(*lengths[:dim], devices, lengths[dim] // devices, *lengths[dim + 1 :])
    return jnp.moveaxis(pieces, dim, 0)


def sum_together(arrays, axis, dims):
    devices = lax.axis_size(axis)
    pieces = [split_up(a, dim, devices) for a, dim in zip(arrays, dims)]
    lines = jnp.concatenate([b.reshape(devices, -1) for b in pieces], axis=1)
    span = max(16, -(-lines.shape[1] // 1024) * 8)
    lines = jnp.pad(lines, ((0, 0), (0, span * 128 - lines.shape[1]))).reshape(-1, 128)
    line, at, outs = (lax.psum_scatter(lines, axis, tiled=True).reshape(-1), 0, [])
    for b in pieces:
        part = b[0]
        outs.append(line[at : at + part.size].reshape(part.shape))
        at += part.size
    return tuple(outs)


def sum_in_order(pieces, axes, sequence):
    lengths = [lax.axis_size(a) for a in axes]
    pieces = pieces.reshape(*lengths, *pieces.shape[1:])
    pieces = pieces.transpose(*sequence, *range(len(axes), pieces.ndim))
    pieces = pieces.reshape(-1, *pieces.shape[len(axes) :])
    for k in sequence:
        pieces = lax.psum_scatter(pieces, axes[k], scatter_dimension=0, tiled=True)
    return pieces[0]


def summed_rows_2(array, axes, sequence, dim):
    devices = lax.axis_size(axes)
    return sum_in_order(split_up(array, dim, devices), axes, sequence)


def apply_norm(raw, norm_gain):
    input_values = raw.astype(jnp.float32)
    inverse_norm = lax.rsqrt(jnp.mean(input_values * input_values, axis=-1, keepdims=True) + EPS)
    unit_input = input_values * inverse_norm
    return (unit_input, inverse_norm, (norm_gain * unit_input).astype(jnp.bfloat16))


def backward_of_norm(incoming_gradient, unit_input, inverse_norm, norm_gain):
    scaled_gradient = norm_gain * incoming_gradient
    mean_correction = jnp.mean(scaled_gradient * unit_input, axis=-1, keepdims=True)
    return inverse_norm * (scaled_gradient - unit_input * mean_correction)


def contract_rows(left, right):
    return lax.dot_general(
        left, right, (((0,), (0,)), ((), ())), preferred_element_type=jnp.float32
    )


def contract_cols(left, right):
    return lax.dot_general(
        left, right, (((1,), (1,)), ((), ())), preferred_element_type=jnp.float32
    )


def body(query_latent, key_value_latent, query_gain, key_value_gain, q_up, kv_up, grad_q, grad_kv):
    query_width = query_latent.shape[1]
    whole_q, whole_kv = one_gather((query_latent, key_value_latent), TENSOR, (0, 0))
    part_q = contract_rows(apply_norm(whole_q, query_gain)[2], grad_q)
    part_kv = contract_rows(apply_norm(whole_kv, key_value_gain)[2], grad_kv)
    d_q_up, d_kv_up = sum_together((part_q, part_kv), "dp", (0, 0))
    summed_products = summed_rows_2(
        jnp.concatenate((contract_cols(grad_q, q_up), contract_cols(grad_kv, kv_up)), axis=1),
        TENSOR,
        (1, 0),
        0,
    )
    query_unit, query_inverse_norm, unused_item = apply_norm(query_latent, query_gain)
    key_value_unit, key_value_inverse_norm, unused_item = apply_norm(
        key_value_latent, key_value_gain
    )
    query_latent_gradient = backward_of_norm(
        summed_products[:, :query_width], query_unit, query_inverse_norm, query_gain
    )
    key_value_latent_gradient = backward_of_norm(
        summed_products[:, query_width:], key_value_unit, key_value_inverse_norm, key_value_gain
    )
    return (query_latent_gradient, key_value_latent_gradient, d_q_up, d_kv_up)


def solution(mesh):
    finer = Mesh(mesh.devices.reshape(mesh.shape["dp"], 2, 32), ("dp", "tensor_0", "tensor_1"))
    placed = (
        P(DP_TENSOR, None),
        P(DP_TENSOR, None),
        P(),
        P(),
        P(None, TENSOR),
        P(None, TENSOR),
        P("dp", TENSOR),
        P("dp", TENSOR),
    )
    return jax.shard_map(
        body,
        mesh=finer,
        in_specs=placed,
        out_specs=(P(DP_TENSOR, None), P(DP_TENSOR, None), P("dp", TENSOR), P("dp", TENSOR)),
        check_vma=False,
    )
```

profile of v0, /device:TPU:8, one launch (start us, length us, event | category | flops | bytes accessed | tf_op | source)
XLA Modules:
  0.0 313.4 jit_solution(1547607393573534996)
XLA Ops:
  8.1 1.5 fusion.19
  9.6 1.4 fusion.18
  11.1 0.6 reshape_reshape.11
  11.7 1.2 copy.14
  13.0 162.3 %all-gather = bf16[262144]{0:T(1024)(128)(2,1)S(1)} all-gather(bf16[4096]{0:T(1024)(128)(2,1)S(1)} %pad_maximum_fusion.2), channel_id=2, replica_groups=mesh['dp'=16,'tensor_0'=2,'tensor_1'=32] {'tensor_0','tensor_1'}, dimensions={0}, use_global_device_ids=true | all-gather | bytes 532480 | tf_op jit(solution)/shard_map/all_gather | solution.py:22
  175.3 0.2 reshape.85
  175.7 0.1 multiply_reduce_fusion.1
  175.8 0.1 reshape.83
  176.0 0.1 multiply_reduce_fusion
  176.1 0.6 add_rsqrt_fusion.1
  176.7 0.4 fusion.3
  177.1 1.2 reshape_reshape.13
  178.3 1.7 fusion
  180.0 1.7 reshape_reshape.12
  181.6 4.0 %pad_maximum_fusion = f32[16,53248]{1,0:T(8,128)} fusion(f32[16,16384]{1,0:T(8,128)} %reshape_reshape.13, f32[16,36864]{1,0:T(8,128)} %reshape_reshape.12), kind=kLoop, calls=%fused_computation | loop fusion | flops 851968 | bytes 6815744 | tf_op jit(solution)/shard_map/concatenate | solution.py:39
  185.6 3.4 %reshape.80 = f32[6656,128]{1,0:T(8,128)} reshape(f32[16,53248]{1,0:T(8,128)} %pad_maximum_fusion) | data formatting | bytes 6815744 | tf_op jit(solution)/shard_map/reshape | solution.py:41
  189.1 1.3 dynamic-slice.2
  190.4 1.3 dynamic-slice
  192.3 0.1 fusion.17
  192.4 0.1 fusion.11
  192.6 95.7 %all-reduce.4.cloned.1.call-done = f32[64,2,2048]{2,1,0:T(2,128)} async-done(((f32[64,2,2048]{2,1,0:T(2,128)}), f32[64,2,2048]{2,1,0:T(2,128)}) %all-reduce.4.cloned.1.call-update) | async-done | bytes 1048592
  288.3 0.8 constant_dynamic-slice_fusion
  289.1 11.3 %all-reduce.1 = f32[2,2,2048]{2,1,0:T(2,128)S(1)} all-reduce(f32[2,2,2048]{2,1,0:T(2,128)S(1)} %constant_dynamic-slice_fusion), channel_id=4, replica_groups=mesh['dp'=16,'tensor_0'=2,'tensor_1'=32] {'tensor_0'}, use_global_device_ids=true, to_apply=%region_2.3.clone | all-reduce | flops 8192 | bytes 65536
  300.4 0.7 dynamic-slice_bitcast_fusion
  301.1 0.2 fusion.14
  301.2 0.2 fusion.8
  301.5 0.7 fusion.16
  302.1 0.7 fusion.10
  302.8 0.9 slice.30
  303.7 0.7 reshape.81
  304.4 0.8 slice.31
  305.3 0.6 reshape.82
  (35 shorter events, 0.4 us)
Async XLA Ops:
  8.0 1.6 copy-start
  8.0 280.3 %all-reduce.4.cloned.1.call-start = ((), (), s32[]{:S(2)}) async-start(), calls=%async_computation.2 | async-start | bytes 2097152
  11.0 1.9 copy-start.5
  11.0 1.9 copy-start.3
  12.9 289.9 %reduce-scatter.2.cloned.1.call-start = ((), (), s32[]{:S(2)}) async-start(), calls=%async_computation.1 | async-start | bytes 3620864 | tf_op jit(solution)/shard_map/reduce_scatter | solution.py:42
  175.5 1.2 copy-start.2
  175.5 1.2 copy-start.7
  175.9 1.2 copy-start.1
  175.9 2.3 copy-start.4
  189.1 3.2 %copy-start.6 = (bf16[2,512]{1,0:T(2,128)(2,1)S(1)}, bf16[2,512]{1,0:T(2,128)(2,1)}, u32[]{:S(2)}) copy-start(bf16[2,512]{1,0:T(2,128)(2,1)} %param.9) | copy-start | bytes 6148
  189.1 112.0 %copy-start.8 = (f32[512]{0:T(512)S(1)}, f32[512]{0:T(512)}, u32[]{:S(2)}) copy-start(f32[512]{0:T(512)} %param.11) | copy-start | bytes 6148
Sparse Core Ops, SparseCore 0:
  13.0 275.2 all-reduce.3
Sparse Core Ops, SparseCore 1:
  189.2 58.9 reduce-scatter.1
where the time goes:
time: 314 us; the launch traced here: 313 us
  blocking collectives  174 us (55%)
  waiting for transfers between devices  95.8 us (31%)
  between operations  16.4 us (5%)
  local copies, waits for them, and re-layouts  15.6 us (5%)
  other arithmetic  6.97 us (2%)
  matrix products  4.99 us (2%)
    all_gather x1, blocking collectives, one_gather(): lines, at, outs = (lax.all_gather(line, axis), 0, [])  162 us
    unnamed x3, waiting for transfers between devices  95.8 us
    unnamed x1, blocking collectives  11.3 us
  transfers between devices with their start and end apart: 2, of which 1 were waited for; matrix products, arithmetic and copies ran while one was open for 6% of the time, Pallas kernels for 0%

commit v1 on v0

v1 whole, which is shorter than its diff:
```python
import jax
import jax.numpy as jnp
from jax import lax
from jax.experimental import pallas as pl
from jax.experimental.pallas import tpu as pltpu
from jax.sharding import PartitionSpec as P

MESH = pl.DeviceIdType.MESH
F32 = jnp.float32
BF16 = jnp.bfloat16
EPS = 1e-06

NEAR = [(1, 0), (2, 0), (3, 0), (0, 1), (1, 1), (2, 1), (3, 1)]
FAR = [1, 7, 2, 6, 3, 5, 4]
PLANE = [(0, 0), (1, 0), (0, 3), (0, 1), (1, 3), (1, 1), (0, 2), (1, 2)]


def iota(shape, dim):
    return lax.broadcasted_iota(jnp.int32, shape, dim)


def one_hot(mask):
    return jnp.where(mask, 1.0, 0.0).astype(BF16)


def dot(a, b, dims):
    return lax.dot_general(a, b, (dims, ((), ())), preferred_element_type=F32)


def kernel(
    ql_hbm, kvl_hbm, qg_hbm, kvg_hbm, qup_hbm, kvup_hbm, gq_hbm, gkv_hbm,
    dql_ref, dkvl_ref, dqup_ref, dkvup_ref,
    ql, kvl, qg, kvg, qup, kvup, grads,
    pack, mixed, piece, gall, xall, part, near_in, send_far, far_in, natural, acc,
    load_sem, mix_send, mix_recv, plane_send, plane_recv, pair_send, pair_recv,
    rnear_send, rnear_recv, rfar_send, rfar_recv, afar_send, afar_recv, anear_send, anear_recv,
    ready,
):
    dp, tensor = lax.axis_index("dp"), lax.axis_index("tensor")
    c = lax.rem(dp, 2)
    y = lax.rem(dp // 2, 4)
    xl = dp // 8
    z = lax.rem(tensor, 32)
    xh = tensor // 32
    r = lax.rem(z, 4)
    j = z // 4
    width = 4 * c - 2
    steps = [0, 1, -1, width]

    def along(dz, flip=0):
        half = 1 - xh if flip else xh
        return (dp, half * 32 + lax.rem(z + dz + 32, 32))

    def chip(dx, dy, other=0):
        px = 1 - xl if dx else xl
        core = 1 - c if other else c
        return (px * 4 + lax.rem(y + dy, 4)) * 2 + core

    barrier = pltpu.get_barrier_semaphore()
    peers = [(lax.rem(dp + k, 16), tensor) for k in range(1, 16)]
    peers += [along(dz, flip) for flip in (0, 1) for dz in (1, -1, 2, -2)]
    peers += [along(0, 1), along(4), along(-4)]
    for peer in peers:
        pl.semaphore_signal(barrier, inc=1, device_id=peer, device_id_type=MESH)

    loads = [
        pltpu.make_async_copy(src, dst, load_sem.at[n])
        for n, (src, dst) in enumerate([
            (ql_hbm, ql), (kvl_hbm, kvl), (qg_hbm, qg), (kvg_hbm, kvg),
            (gq_hbm, grads.at[:, 0:384]), (gkv_hbm, grads.at[:, 384:896]),
            (qup_hbm, qup), (kvup_hbm, kvup),
        ])
    ]
    for load in loads:
        load.start()
    sent = []

    def send(src, dst, send_sem, recv_sem, device):
        copy = pltpu.make_async_remote_copy(
            src_ref=src, dst_ref=dst, send_sem=send_sem, recv_sem=recv_sem,
            device_id=device, device_id_type=MESH)
        copy.start()
        return copy

    for load in loads[:4]:
        load.wait()

    def norm(raw, gain):
        wide = raw[...].astype(F32)
        inverse = lax.rsqrt(jnp.mean(wide * wide, axis=-1, keepdims=True) + EPS)
        unit = wide * inverse
        return unit, inverse, gain[...] * unit

    q_unit, q_inv, q_normed = norm(ql, qg)
    kv_unit, kv_inv, kv_normed = norm(kvl, kvg)
    for b in range(16):
        pack[b, :, 0:96] = q_normed[:, 96 * b : 96 * b + 96]
        pack[b, :, 96:128] = kv_normed[:, 32 * b : 32 * b + 32]

    for load in loads[4:6]:
        load.wait()
    row, col = iota((128, 128), 0), iota((128, 128), 1)
    token = ((row >> 4) & 1) * 64 + ((row >> 1) & 7) * 8 + (row >> 5) * 2 + (row & 1)
    order = one_hot(col == token)
    ordered = dot(order, grads[...], ((1,), (0,))).astype(BF16)
    gall[dp] = ordered.reshape(4, 2, 16, 896)
    mixed[dp] = pack[dp]

    pl.semaphore_wait(barrier, len(peers))
    pl.semaphore_signal(ready.at[0], inc=1, device_id=along(-4), device_id_type=MESH)
    pl.semaphore_signal(ready.at[1], inc=1, device_id=along(4), device_id_type=MESH)

    mixes = []
    for k in range(1, 16):
        to = lax.rem(dp + k, 16)
        mixes.append(send(pack.at[to], mixed.at[dp], mix_send.at[k], mix_recv.at[k], (to, tensor)))

    def relay(n, dx, dy):
        return gall.at[chip(*PLANE[n])]

    def pass_on(n, slot, dx, dy):
        at = gall.at[chip(*PLANE[n])]
        return send(at, at, plane_send.at[slot], plane_recv.at[slot], (chip(dx, dy), tensor))

    def to_pair(n):
        at = gall.at[chip(*PLANE[n])]
        return send(at, at, pair_send.at[n], pair_recv.at[n], (chip(0, 0, 1), tensor))

    plane = {}
    plane[1] = pass_on(0, 1, 1, 0)
    plane[2] = pass_on(0, 2, 0, 1)
    plane[3] = pass_on(0, 3, 0, 3)
    pairs = [to_pair(0)]

    loads[6].wait()
    loads[7].wait()
    own = gall[dp].reshape(128, 896)
    for q in range(4):
        if q < 3:
            value = dot(own[:, 0:384], qup[512 * q : 512 * q + 512, :], ((1,), (1,)))
        else:
            value = dot(own[:, 384:896], kvup[...], ((1,), (1,)))
        part[:, :, q] = value.astype(BF16).reshape(4, 2, 16, 512)

    rnear = []
    for n, (s, flip) in enumerate(NEAR):
        device = along(steps[s], flip)
        half = 1 - xh if flip else xh
        cls = lax.rem(z + steps[s] + 32, 4)
        rnear.append(send(part.at[cls, half], near_in.at[n], rnear_send.at[n], rnear_recv.at[n], device))

    pl.semaphore_wait(ready.at[0], 1)
    pl.semaphore_wait(ready.at[1], 1)
    pl.semaphore_signal(ready.at[2], inc=1, device_id=along(-8), device_id_type=MESH)
    pl.semaphore_signal(ready.at[3], inc=1, device_id=along(8), device_id_type=MESH)

    for copy in mixes:
        copy.wait_recv()
    for b in range(16):
        piece[2 * b : 2 * b + 2, :] = mixed[b]
    xall[xh, r, j] = piece[...].astype(BF16)

    def far_send(k):
        at = xall.at[xh, r, j]
        return send(at, at, afar_send.at[k], afar_recv.at[k], along(4 * k))

    def near_forward(k):
        at = xall.at[xh, r, lax.rem(j + 8 - k, 8)]
        for n, (s, flip) in enumerate(NEAR):
            send(at, at, anear_send.at[n], anear_recv.at[n], along(steps[s], flip))

    afar = {}
    for k in FAR[:4]:
        afar[k] = far_send(k)
    near_forward(0)
    pl.semaphore_wait(ready.at[2], 1)
    pl.semaphore_wait(ready.at[3], 1)
    for k in FAR[4:]:
        afar[k] = far_send(k)

    plane[1].wait_recv()
    plane[4] = pass_on(1, 4, 0, 1)
    plane[5] = pass_on(1, 5, 0, 3)
    pairs.append(to_pair(1))
    plane[2].wait_recv()
    plane[6] = pass_on(2, 6, 0, 1)
    pairs.append(to_pair(2))
    plane[3].wait_recv()
    pairs.append(to_pair(3))

    for k in FAR[:2]:
        afar[k].wait_recv()
        near_forward(k)

    for copy in rnear:
        copy.wait_recv()
    total = part[r, xh].astype(F32)
    for n in range(7):
        total = total + near_in[n].astype(F32)
    row, col = iota((64, 64), 0), iota((64, 64), 1)
    spread = one_hot(col == (row & 3) * 16 + (row >> 3) * 2 + ((row >> 2) & 1))
    total = dot(spread, total.astype(BF16).reshape(64, 512), ((1,), (0,)))
    send_far[...] = total.astype(BF16).reshape(8, 8, 512)

    for k in FAR[2:4]:
        afar[k].wait_recv()
        near_forward(k)

    rfar = []
    for k in FAR:
        rfar.append(send(send_far.at[lax.rem(j + k, 8)], far_in.at[k], rfar_send.at[k], rfar_recv.at[k], along(4 * k)))

    plane[4].wait_recv()
    pairs.append(to_pair(4))
    plane[5].wait_recv()
    plane[7] = pass_on(5, 7, 0, 3)
    pairs.append(to_pair(5))
    plane[6].wait_recv()
    pairs.append(to_pair(6))

    for k in FAR[4:]:
        afar[k].wait_recv()
        near_forward(k)
    plane[7].wait_recv()
    pairs.append(to_pair(7))
    for copy in pairs:
        copy.wait_recv()

    row, col = iota((256, 256), 0), iota((256, 256), 1)
    regroup = one_hot(col == ((row >> 1) & 15) * 16 + (row >> 5) * 2 + (row & 1))

    def weights(half, cls):
        x = dot(xall[half, cls].reshape(256, 128), regroup, ((0,), (0,))).astype(BF16)
        g = gall[:, cls, half].reshape(256, 896)
        return dot(x, g, ((1,), (0,)))

    acc[...] = weights(xh, r)

    for copy in rfar:
        copy.wait_recv()
    latent = send_far[j].astype(F32)
    for k in range(1, 8):
        latent = latent + far_in[k].astype(F32)
    for i in range(2):
        for q in range(4):
            natural[i : i + 1, 512 * q : 512 * q + 512] = latent[4 * i + q : 4 * i + q + 1, :]

    def norm_back(incoming, unit, inverse, gain):
        scaled = gain[...] * incoming
        mean = jnp.mean(scaled * unit, axis=-1, keepdims=True)
        return inverse * (scaled - unit * mean)

    q_unit, q_inv, q_normed = norm(ql, qg)
    kv_unit, kv_inv, kv_normed = norm(kvl, kvg)
    dql_ref[...] = norm_back(natural[:, 0:1536], q_unit, q_inv, qg)
    dkvl_ref[...] = norm_back(natural[:, 1536:2048], kv_unit, kv_inv, kvg)

    for n, (s, flip) in enumerate(NEAR):
        half = 1 - xh if flip else xh
        cls = lax.rem(z - steps[s] + 32, 4)
        whole = xall.at[half, cls]
        pltpu.make_async_remote_copy(
            src_ref=whole, dst_ref=whole, send_sem=anear_send.at[n], recv_sem=anear_recv.at[n],
            device_id=along(steps[s], flip), device_id_type=MESH).wait_recv()
        acc[...] += weights(half, cls)
    dqup_ref[...] = acc[0:96, 0:384]
    dkvup_ref[...] = acc[96:128, 384:896]

    for copy in mixes + list(plane.values()) + pairs + rnear + rfar + list(afar.values()):
        copy.wait_send()
    for n, (s, flip) in enumerate(NEAR):
        whole = xall.at[xh, r]
        pltpu.make_async_remote_copy(
            src_ref=whole, dst_ref=whole, send_sem=anear_send.at[n], recv_sem=anear_recv.at[n],
            device_id=along(steps[s], flip), device_id_type=MESH).wait_send()


def body(query_latent, key_value_latent, query_gain, key_value_gain, q_up, kv_up, grad_q, grad_kv):
    dma = pltpu.SemaphoreType.DMA
    vmem = pltpu.VMEM
    return pl.pallas_call(
        kernel,
        name="mla_up_backward",
        out_shape=(
            jax.ShapeDtypeStruct((2, 1536), F32),
            jax.ShapeDtypeStruct((2, 512), F32),
            jax.ShapeDtypeStruct((96, 384), F32),
            jax.ShapeDtypeStruct((32, 512), F32),
        ),
        in_specs=[pl.BlockSpec(memory_space=pltpu.HBM)] * 8,
        out_specs=(pl.BlockSpec(memory_space=pltpu.VMEM),) * 4,
        scratch_shapes=[
            vmem((2, 1536), BF16), vmem((2, 512), BF16), vmem((1, 1536), F32), vmem((1, 512), F32),
            vmem((1536, 384), BF16), vmem((512, 512), BF16), vmem((128, 896), BF16),
            vmem((16, 2, 128), F32),
            vmem((16, 2, 128), F32),
            vmem((32, 128), F32),
            vmem((16, 4, 2, 16, 896), BF16),
            vmem((2, 4, 8, 32, 128), BF16),
            vmem((4, 2, 4, 16, 512), BF16),
            vmem((7, 4, 16, 512), BF16),
            vmem((8, 8, 512), BF16),
            vmem((8, 8, 512), BF16),
            vmem((2, 2048), F32),
            vmem((128, 896), F32),
            dma((8,)), dma((16,)), dma((16,)), dma((8,)), dma((8,)), dma((8,)), dma((8,)),
            dma((7,)), dma((7,)), dma((8,)), dma((8,)), dma((8,)), dma((8,)), dma((7,)), dma((7,)),
            pltpu.SemaphoreType.REGULAR((4,)),
        ],
        compiler_params=pltpu.CompilerParams(
            collective_id=0, has_side_effects=True, vmem_limit_bytes=48 * 1024 * 1024),
    )(query_latent, key_value_latent, query_gain.reshape(1, -1), key_value_gain.reshape(1, -1), q_up, kv_up, grad_q, grad_kv)


def solution(mesh):
    group = ("dp", "tensor")
    placed = (
        P(group, None), P(group, None), P(), P(), P(None, "tensor"), P(None, "tensor"),
        P("dp", "tensor"), P("dp", "tensor"),
    )
    return jax.shard_map(
        body,
        mesh=mesh,
        in_specs=placed,
        out_specs=(P(group, None), P(group, None), P("dp", "tensor"), P("dp", "tensor")),
        check_vma=False,
    )
```

time: 314 us -> 68.2 us (0.22)
  the two profiles are of different devices: /device:TPU:8 before, /device:TPU:1 now
where the time goes in v1:
time: 68.2 us; the launch traced here: 66.9 us
  Pallas kernels  56.9 us (83%)
  local copies, waits for them, and re-layouts  9.35 us (14%)
    pallas_call x1, Pallas kernels, body(): pl.pallas_call(kernel, name='mla_up_backward', out_shape=(jax.ShapeDtypeS...  56.9 us
    unnamed x18, local copies, waits for them, and re-layouts  8.64 us

profile of v1, /device:TPU:1, one launch (start us, length us, event | category | flops | bytes accessed | tf_op | source)
XLA Modules:
  0.0 66.9 jit_solution(9891508986359082825)
XLA Ops:
  0.6 0.7 %reshape.14.qg_hbm = f32[1,1536]{1,0:T(1,128)S(1)} reshape(f32[1536]{0:T(1024)} %param.10) | data formatting | bytes 12288 | tf_op jit(solution)/shard_map/reshape | solution.py:312
  1.3 0.0 copy-start
  1.3 1.3 %copy-done = bf16[1536,384]{1,0:T(8,128)(2,1)S(1)} copy-done((bf16[1536,384]{1,0:T(8,128)(2,1)S(1)}, bf16[1536,384]{1,0:T(8,128)(2,1)}, u32[]{:S(2)}) %copy-start) | copy-done | bytes 1179672
  2.6 0.0 copy-start.1
  2.6 1.0 %copy-done.1 = bf16[512,512]{1,0:T(8,128)(2,1)S(1)} copy-done((bf16[512,512]{1,0:T(8,128)(2,1)S(1)}, bf16[512,512]{1,0:T(8,128)(2,1)}, u32[]{:S(2)}) %copy-start.1) | copy-done | bytes 524312
  3.6 0.0 copy-start.2
  3.6 0.9 %copy-done.2 = bf16[128,512]{1,0:T(8,128)(2,1)S(1)} copy-done((bf16[128,512]{1,0:T(8,128)(2,1)S(1)}, bf16[128,512]{1,0:T(8,128)(2,1)}, u32[]{:S(2)}) %copy-start.2) | copy-done | bytes 131096
  4.6 0.0 copy-start.3
  4.6 0.9 %copy-done.3 = bf16[128,384]{1,0:T(8,128)(2,1)S(1)} copy-done((bf16[128,384]{1,0:T(8,128)(2,1)S(1)}, bf16[128,384]{1,0:T(8,128)(2,1)}, u32[]{:S(2)}) %copy-start.3) | copy-done | bytes 98328
  5.4 0.0 copy-start.4
  5.4 0.7 %copy-done.4 = bf16[2,1536]{1,0:T(2,128)(2,1)S(1)} copy-done((bf16[2,1536]{1,0:T(2,128)(2,1)S(1)}, bf16[2,1536]{1,0:T(2,128)(2,1)}, u32[]{:S(2)}) %copy-start.4) | copy-done | bytes 6168
  6.1 0.0 copy-start.5
  6.1 0.7 %copy-done.5 = bf16[2,512]{1,0:T(2,128)(2,1)S(1)} copy-done((bf16[2,512]{1,0:T(2,128)(2,1)S(1)}, bf16[2,512]{1,0:T(2,128)(2,1)}, u32[]{:S(2)}) %copy-start.5) | copy-done | bytes 2072
  6.8 0.0 copy-start.6
  6.8 0.7 %copy-done.6 = f32[512]{0:T(512)S(1)} copy-done((f32[512]{0:T(512)S(1)}, f32[512]{0:T(512)}, u32[]{:S(2)}) %copy-start.6) | copy-done | bytes 2072
  7.5 56.9 %mla_up_backward.1 = (f32[2,1536]{1,0:T(2,128)S(1)}, f32[2,512]{1,0:T(2,128)S(1)}, f32[96,384]{1,0:T(8,128)S(1)}, f32[32,512]{1,0:T(8,128)S(1)}) custom-call(bf16[2,1536]{1,0:T(2,128)(2,1)S(1)} %copy-done.4, bf16[2,512]{1,0:T(2,128)(2,1)S(1)} %copy-done.5, f32[1,1536]{1,0:T(1,128)S(1)} %reshape.14.qg_hbm, f32[1,512]{1,0:T(1,128)S(1)} %bitcast.1, ...), custom_call_target="tpu_custom_call" | custom-call | tf_op jit(solution)/shard_map/mla_up_backward/pallas_call | solution.py:281
  64.4 0.6 copy.16
  65.0 0.6 copy.17
  65.6 0.7 copy.18
  66.2 0.6 copy.19
Async XLA Ops:
  1.3 1.3 %copy-start = (bf16[1536,384]{1,0:T(8,128)(2,1)S(1)}, bf16[1536,384]{1,0:T(8,128)(2,1)}, u32[]{:S(2)}) copy-start(bf16[1536,384]{1,0:T(8,128)(2,1)} %qup_hbm.1) | copy-start | bytes 3538948
  2.6 1.0 %copy-start.1 = (bf16[512,512]{1,0:T(8,128)(2,1)S(1)}, bf16[512,512]{1,0:T(8,128)(2,1)}, u32[]{:S(2)}) copy-start(bf16[512,512]{1,0:T(8,128)(2,1)} %kvup_hbm.1) | copy-start | bytes 1572868
  3.6 0.9 %copy-start.2 = (bf16[128,512]{1,0:T(8,128)(2,1)S(1)}, bf16[128,512]{1,0:T(8,128)(2,1)}, u32[]{:S(2)}) copy-start(bf16[128,512]{1,0:T(8,128)(2,1)} %gkv_hbm.1) | copy-start | bytes 393220
  4.6 0.9 %copy-start.3 = (bf16[128,384]{1,0:T(8,128)(2,1)S(1)}, bf16[128,384]{1,0:T(8,128)(2,1)}, u32[]{:S(2)}) copy-start(bf16[128,384]{1,0:T(8,128)(2,1)} %gq_hbm.1) | copy-start | bytes 294916
  5.4 0.7 %copy-start.4 = (bf16[2,1536]{1,0:T(2,128)(2,1)S(1)}, bf16[2,1536]{1,0:T(2,128)(2,1)}, u32[]{:S(2)}) copy-start(bf16[2,1536]{1,0:T(2,128)(2,1)} %ql_hbm.1) | copy-start | bytes 18436
  6.1 0.7 %copy-start.5 = (bf16[2,512]{1,0:T(2,128)(2,1)S(1)}, bf16[2,512]{1,0:T(2,128)(2,1)}, u32[]{:S(2)}) copy-start(bf16[2,512]{1,0:T(2,128)(2,1)} %kvl_hbm.1) | copy-start | bytes 6148
  6.8 0.7 %copy-start.6 = (f32[512]{0:T(512)S(1)}, f32[512]{0:T(512)}, u32[]{:S(2)}) copy-start(f32[512]{0:T(512)} %param.11) | copy-start | bytes 6148

commit v2 on v1

v2 whole, which is shorter than its diff:
```python
import jax
import jax.numpy as jnp
from jax import lax
from jax.experimental import pallas as pl
from jax.experimental.pallas import tpu as pltpu
from jax.sharding import PartitionSpec as P

MESH = pl.DeviceIdType.MESH
F32 = jnp.float32
BF16 = jnp.bfloat16
EPS = 1e-06
scope = jax.named_scope

NEAR = [(1, 0), (2, 0), (3, 0), (0, 1), (1, 1), (2, 1), (3, 1)]
FAR = [1, 7, 2, 6, 3, 5, 4]
PLANE = [(0, 0), (1, 0), (0, 3), (0, 1), (1, 3), (1, 1), (0, 2), (1, 2)]


def iota(shape, dim):
    return lax.broadcasted_iota(jnp.int32, shape, dim)


def one_hot(mask):
    return jnp.where(mask, 1.0, 0.0).astype(BF16)


def dot(a, b, dims):
    return lax.dot_general(a, b, (dims, ((), ())), preferred_element_type=F32)


def kernel(
    ql_hbm, kvl_hbm, qg_hbm, kvg_hbm, qup_hbm, kvup_hbm, gq_hbm, gkv_hbm,
    dql_hbm, dkvl_hbm, dqup_hbm, dkvup_hbm,
    ql, kvl, qg, kvg, qup, kvup, grads,
    pack, mixed, piece, gall, xall, part, near_in, send_far, far_in, natural, acc,
    load_sem, mix_send, mix_recv, plane_send, plane_recv, pair_send, pair_recv,
    rnear_send, rnear_recv, rfar_send, rfar_recv, afar_send, afar_recv, anear_send, anear_recv,
    dql, dkvl, out_sem, ready,
):
    dp, tensor = lax.axis_index("dp"), lax.axis_index("tensor")
    c = lax.rem(dp, 2)
    y = lax.rem(dp // 2, 4)
    xl = dp // 8
    z = lax.rem(tensor, 32)
    xh = tensor // 32
    r = lax.rem(z, 4)
    j = z // 4
    width = 4 * c - 2
    steps = [0, 1, -1, width]

    def along(dz, flip=0):
        half = 1 - xh if flip else xh
        return (dp, half * 32 + lax.rem(z + dz + 32, 32))

    def chip(dx, dy, other=0):
        px = 1 - xl if dx else xl
        core = 1 - c if other else c
        return (px * 4 + lax.rem(y + dy, 4)) * 2 + core

    barrier = pltpu.get_barrier_semaphore()
    peers = [along(4), along(-4)]
    peers += [along(dz, flip) for flip in (1, 0) for dz in (2, -2, 1, -1)]
    peers += [(lax.rem(dp + k, 16), tensor) for k in range(15, 0, -1)]
    peers += [along(0, 1)]
    for peer in peers:
        pl.semaphore_signal(barrier, inc=1, device_id=peer, device_id_type=MESH)

    loads = [
        pltpu.make_async_copy(src, dst, load_sem.at[n])
        for n, (src, dst) in enumerate([
            (ql_hbm, ql), (kvl_hbm, kvl), (qg_hbm, qg), (kvg_hbm, kvg),
            (gq_hbm, grads.at[:, 0:384]), (gkv_hbm, grads.at[:, 384:896]),
            (qup_hbm, qup), (kvup_hbm, kvup),
        ])
    ]
    for load in loads:
        load.start()
    sent = []

    def send(src, dst, send_sem, recv_sem, device):
        copy = pltpu.make_async_remote_copy(
            src_ref=src, dst_ref=dst, send_sem=send_sem, recv_sem=recv_sem,
            device_id=device, device_id_type=MESH)
        copy.start()
        return copy

    with scope("w_loadsmall"):
        for load in loads[:4]:
            load.wait()

    def norm(raw, gain):
        wide = raw[...].astype(F32)
        inverse = lax.rsqrt(jnp.mean(wide * wide, axis=-1, keepdims=True) + EPS)
        unit = wide * inverse
        return unit, inverse, gain[...].reshape(1, -1) * unit

    q_unit, q_inv, q_normed = norm(ql, qg)
    kv_unit, kv_inv, kv_normed = norm(kvl, kvg)
    for b in range(16):
        pack[b, :, 0:96] = q_normed[:, 96 * b : 96 * b + 96]
        pack[b, :, 96:128] = kv_normed[:, 32 * b : 32 * b + 32]

    with scope("w_loadgrads"):
        for load in loads[4:6]:
            load.wait()
    row, col = iota((128, 128), 0), iota((128, 128), 1)
    token = ((row >> 4) & 1) * 64 + ((row >> 1) & 7) * 8 + (row >> 5) * 2 + (row & 1)
    order = one_hot(col == token)
    ordered = dot(order, grads[...], ((1,), (0,))).astype(BF16)
    gall[dp] = ordered.reshape(4, 2, 16, 896)
    mixed[dp] = pack[dp]

    with scope("w_loadup"):
        loads[6].wait()
        loads[7].wait()
    own = gall[dp].reshape(128, 896)
    for q in range(4):
        if q < 3:
            value = dot(own[:, 0:384], qup[512 * q : 512 * q + 512, :], ((1,), (1,)))
        else:
            value = dot(own[:, 384:896], kvup[...], ((1,), (1,)))
        part[:, :, q] = value.astype(BF16).reshape(4, 2, 16, 512)

    with scope("w_barrier"):
        pl.semaphore_wait(barrier, len(peers))
    pl.semaphore_signal(ready.at[0], inc=1, device_id=along(-4), device_id_type=MESH)
    pl.semaphore_signal(ready.at[1], inc=1, device_id=along(4), device_id_type=MESH)

    mixes = []
    for k in range(1, 16):
        to = lax.rem(dp + k, 16)
        mixes.append(send(pack.at[to], mixed.at[dp], mix_send.at[k], mix_recv.at[k], (to, tensor)))

    whole, low, high = pl.ds(0, 4), pl.ds(0, 2), pl.ds(2, 2)

    def pass_on(n, slot, dx, dy, rows=whole):
        at = gall.at[chip(*PLANE[n]), rows]
        return send(at, at, plane_send.at[slot], plane_recv.at[slot], (chip(dx, dy), tensor))

    def to_pair(n, slot, rows=whole):
        at = gall.at[chip(*PLANE[n]), rows]
        return send(at, at, pair_send.at[slot], pair_recv.at[slot], (chip(0, 0, 1), tensor))

    rnear = []
    for n, (s, flip) in enumerate(NEAR):
        device = along(steps[s], flip)
        half = 1 - xh if flip else xh
        cls = lax.rem(z + steps[s] + 32, 4)
        rnear.append(send(part.at[cls, half], near_in.at[n], rnear_send.at[n], rnear_recv.at[n], device))

    plane = {}
    plane[2] = pass_on(0, 2, 0, 1)
    plane[3] = pass_on(0, 3, 0, 3)
    plane[1] = pass_on(0, 1, 1, 0)
    pairs = [to_pair(0, 0)]

    with scope("w_ready01"):
        pl.semaphore_wait(ready.at[0], 1)
        pl.semaphore_wait(ready.at[1], 1)
    pl.semaphore_signal(ready.at[2], inc=1, device_id=along(-8), device_id_type=MESH)
    pl.semaphore_signal(ready.at[3], inc=1, device_id=along(8), device_id_type=MESH)

    with scope("w_mixes"):
        for copy in mixes:
            copy.wait_recv()
    for b in range(16):
        piece[2 * b : 2 * b + 2, :] = mixed[b]
    xall[xh, r, j] = piece[...].astype(BF16)

    def far_pass(k, slot, dz):
        at = xall.at[xh, r, lax.rem(j + 8 - k, 8)]
        return send(at, at, afar_send.at[slot], afar_recv.at[slot], along(dz))

    def near_forward(k):
        at = xall.at[xh, r, lax.rem(j + 8 - k, 8)]
        for n, (s, flip) in enumerate(NEAR):
            send(at, at, anear_send.at[n], anear_recv.at[n], along(steps[s], flip))

    afar = {}
    afar[2] = far_pass(0, 2, 8)
    afar[6] = far_pass(0, 6, -8)
    afar[1] = far_pass(0, 1, 4)
    afar[7] = far_pass(0, 7, -4)
    near_forward(0)

    def await_plane(*slots):
        for slot in slots:
            with scope(f"w_plane{slot}"):
                plane[slot].wait_recv()

    def await_far(*slots):
        for slot in slots:
            with scope(f"w_afar{slot}"):
                afar[slot].wait_recv()

    await_plane(2)
    plane[6] = pass_on(2, 6, 0, 1, low)
    pairs.append(to_pair(2, 2))
    await_plane(3)
    plane[8] = pass_on(3, 8, 0, 3, high)
    pairs.append(to_pair(3, 3))
    for n, copy in enumerate(rnear):
        with scope(f"w_rnear{n}"):
            copy.wait_recv()
    total = part[r, xh].astype(F32)
    for n in range(7):
        total = total + near_in[n].astype(F32)
    row, col = iota((64, 64), 0), iota((64, 64), 1)
    spread = one_hot(col == (row & 3) * 16 + (row >> 3) * 2 + ((row >> 2) & 1))
    total = dot(spread, total.astype(BF16).reshape(64, 512), ((1,), (0,)))
    send_far[...] = total.astype(BF16).reshape(8, 8, 512)

    with scope("w_ready23"):
        pl.semaphore_wait(ready.at[2], 1)
        pl.semaphore_wait(ready.at[3], 1)
    rfar = {}

    def far_sums(*slots):
        for k in slots:
            rfar[k] = send(send_far.at[lax.rem(j + k, 8)], far_in.at[k], rfar_send.at[k], rfar_recv.at[k], along(4 * k))

    far_sums(4, 3, 5)
    await_far(1)
    near_forward(1)
    await_far(7)
    near_forward(7)
    await_far(2)
    afar[4] = far_pass(2, 4, 8)
    afar[3] = far_pass(2, 3, 4)
    near_forward(2)
    await_far(6)
    afar[5] = far_pass(6, 5, -4)
    far_sums(2, 6, 1, 7)
    near_forward(6)

    await_plane(1)
    plane[4] = pass_on(1, 4, 0, 1)
    plane[5] = pass_on(1, 5, 0, 3)
    pairs.append(to_pair(1, 1))

    await_plane(6)
    plane[7] = pass_on(6, 7, 1, 0, low)
    await_plane(8)
    plane[9] = pass_on(6, 9, 1, 0, high)
    pairs.append(to_pair(6, 6))

    await_far(3)
    near_forward(3)
    await_far(5)
    near_forward(5)

    await_plane(4)
    pairs.append(to_pair(4, 4))
    await_plane(5)
    pairs.append(to_pair(5, 5))
    await_far(4)
    near_forward(4)
    await_plane(7)
    pairs.append(to_pair(7, 7, low))
    await_plane(9)
    pairs.append(to_pair(7, 8, high))
    with scope("w_pairs"):
        for copy in pairs:
            copy.wait_recv()

    row, col = iota((256, 256), 0), iota((256, 256), 1)
    regroup = one_hot(col == ((row >> 1) & 15) * 16 + (row >> 5) * 2 + (row & 1))

    def weights(half, cls):
        x = dot(xall[half, cls].reshape(256, 128), regroup, ((0,), (0,))).astype(BF16)
        g = gall[:, cls, half].reshape(256, 896)
        return dot(x, g, ((1,), (0,)))

    acc[...] = weights(xh, r)

    for k in FAR:
        with scope(f"w_rfar{k}"):
            rfar[k].wait_recv()
    latent = send_far[j].astype(F32)
    for k in range(1, 8):
        latent = latent + far_in[k].astype(F32)
    for i in range(2):
        for q in range(4):
            natural[i : i + 1, 512 * q : 512 * q + 512] = latent[4 * i + q : 4 * i + q + 1, :]

    def norm_back(incoming, unit, inverse, gain):
        scaled = gain[...].reshape(1, -1) * incoming
        mean = jnp.mean(scaled * unit, axis=-1, keepdims=True)
        return inverse * (scaled - unit * mean)

    q_unit, q_inv, q_normed = norm(ql, qg)
    kv_unit, kv_inv, kv_normed = norm(kvl, kvg)
    dql[...] = norm_back(natural[:, 0:1536], q_unit, q_inv, qg)
    dkvl[...] = norm_back(natural[:, 1536:2048], kv_unit, kv_inv, kvg)

    outs = [
        pltpu.make_async_copy(src, dst, out_sem.at[n])
        for n, (src, dst) in enumerate([
            (dql, dql_hbm), (dkvl, dkvl_hbm), (acc.at[0:96, 0:384], dqup_hbm), (acc.at[96:128, 384:896], dkvup_hbm)])
    ]
    outs[0].start()
    outs[1].start()

    def near_copy(n, at):
        s, flip = NEAR[n]
        return pltpu.make_async_remote_copy(
            src_ref=at, dst_ref=at, send_sem=anear_send.at[n], recv_sem=anear_recv.at[n],
            device_id=along(steps[s], flip), device_id_type=MESH)

    places = []
    for n, (s, flip) in enumerate(NEAR):
        half = 1 - xh if flip else xh
        cls = lax.rem(z - steps[s] + 32, 4)
        places.append((half, cls))
        with scope(f"w_anear{n}"):
            near_copy(n, xall.at[half, cls]).wait_recv()
    with scope("c_weights"):
        total = acc[...]
        for half, cls in places:
            total = total + weights(half, cls)
        acc[...] = total
    outs[2].start()
    outs[3].start()

    with scope("w_sends"):
        for copy in mixes + list(plane.values()) + pairs + rnear + list(rfar.values()) + list(afar.values()):
            copy.wait_send()
        for n in range(7):
            near_copy(n, xall.at[xh, r]).wait_send()
    with scope("w_outs"):
        for out in outs:
            out.wait()


def write_kernel(a, b, w, v, dql, dkvl, dqup, dkvup, at, bt, wt, vt, sem_in, sem_out):
    stages = list(enumerate([(w, wt, dqup), (v, vt, dkvup), (a, at, dql), (b, bt, dkvl)]))
    ins = [pltpu.make_async_copy(src, mid, sem_in.at[n]) for n, (src, mid, dst) in stages]
    outs = [pltpu.make_async_copy(mid, dst, sem_out.at[n]) for n, (src, mid, dst) in stages]
    for copy in ins:
        copy.start()
    for copy, out in zip(ins, outs):
        copy.wait()
        out.start()
    for out in outs:
        out.wait()


def body(query_latent, key_value_latent, query_gain, key_value_gain, q_up, kv_up, grad_q, grad_kv):
    dma = pltpu.SemaphoreType.DMA
    vmem = pltpu.VMEM
    hbm = pl.BlockSpec(memory_space=pltpu.HBM)
    shapes = (
        jax.ShapeDtypeStruct((2, 1536), F32),
        jax.ShapeDtypeStruct((2, 512), F32),
        jax.ShapeDtypeStruct((96, 384), F32),
        jax.ShapeDtypeStruct((32, 512), F32),
    )
    results = pl.pallas_call(
        kernel,
        name="mla_up_backward",
        out_shape=shapes,
        in_specs=[hbm] * 8,
        out_specs=(hbm,) * 4,
        scratch_shapes=[
            vmem((2, 1536), BF16), vmem((2, 512), BF16), vmem((1536,), F32), vmem((512,), F32),
            vmem((1536, 384), BF16), vmem((512, 512), BF16), vmem((128, 896), BF16),
            vmem((16, 2, 128), F32),
            vmem((16, 2, 128), F32),
            vmem((32, 128), F32),
            vmem((16, 4, 2, 16, 896), BF16),
            vmem((2, 4, 8, 32, 128), BF16),
            vmem((4, 2, 4, 16, 512), BF16),
            vmem((7, 4, 16, 512), BF16),
            vmem((8, 8, 512), BF16),
            vmem((8, 8, 512), BF16),
            vmem((2, 2048), F32),
            vmem((128, 896), F32),
            dma((8,)), dma((16,)), dma((16,)), dma((10,)), dma((10,)), dma((9,)), dma((9,)),
            dma((7,)), dma((7,)), dma((8,)), dma((8,)), dma((8,)), dma((8,)), dma((7,)), dma((7,)),
            vmem((2, 1536), F32), vmem((2, 512), F32), dma((4,)),
            pltpu.SemaphoreType.REGULAR((4,)),
        ],
        compiler_params=pltpu.CompilerParams(
            collective_id=0, has_side_effects=True, vmem_limit_bytes=67043328),
    )(query_latent, key_value_latent, query_gain, key_value_gain, q_up, kv_up, grad_q, grad_kv)
    return pl.pallas_call(
        write_kernel,
        name="write_results",
        out_shape=shapes,
        in_specs=[hbm] * 4,
        out_specs=(hbm,) * 4,
        scratch_shapes=[vmem(shape.shape, F32) for shape in shapes] + [dma((4,)), dma((4,))],
        compiler_params=pltpu.CompilerParams(vmem_limit_bytes=67043328),
    )(*results)


def solution(mesh):
    group = ("dp", "tensor")
    placed = (
        P(group, None), P(group, None), P(), P(), P(None, "tensor"), P(None, "tensor"),
        P("dp", "tensor"), P("dp", "tensor"),
    )
    return jax.shard_map(
        body,
        mesh=mesh,
        in_specs=placed,
        out_specs=(P(group, None), P(group, None), P("dp", "tensor"), P("dp", "tensor")),
        check_vma=False,
    )
```

time: 68.2 us -> 58.1 us (0.85); the launches traced: 66.9 us -> 57.9 us
  local copies, waits for them, and re-layouts: 9.35 us -> 0 us
    unnamed x18 -> x0, local copies, waits for them, and re-layouts: 8.64 us -> none
    reshape x1 -> x0, local copies, waits for them, and re-layouts: 0.7 us -> none  [body(): query_gain.reshape(1, -1)]
    pallas_call x1 -> x2, Pallas kernels: 56.9 us -> 57.2 us  [the longest x1 55.6 us: body(): pl.pallas_call(kernel, name='mla_up_backward', out_shape=shapes, in_specs...]
where the time goes in v2:
time: 58.1 us; the launch traced here: 57.9 us
  Pallas kernels  57.2 us (98%)
  between operations  0.64 us (1%)
    pallas_call x1, Pallas kernels, body(): pl.pallas_call(kernel, name='mla_up_backward', out_shape=shapes, in_specs...  55.6 us
    pallas_call x1, Pallas kernels, body(): pl.pallas_call(write_kernel, name='write_results', out_shape=shapes, in_s...  1.66 us

profile of v2, /device:TPU:1, one launch (start us, length us, event | category | flops | bytes accessed | tf_op | source)
XLA Modules:
  0.0 57.9 jit_solution(2037190257898067977)
XLA Ops:
  0.6 55.6 %mla_up_backward.1 = (f32[2,1536]{1,0:T(2,128)}, f32[2,512]{1,0:T(2,128)}, f32[96,384]{1,0:T(8,128)}, f32[32,512]{1,0:T(8,128)}) custom-call(bf16[2,1536]{1,0:T(2,128)(2,1)} %ql_hbm.1, bf16[2,512]{1,0:T(2,128)(2,1)} %kvl_hbm.1, f32[1536]{0:T(1024)} %qg_hbm.1, f32[512]{0:T(512)} %kvg_hbm.1, bf16[1536,384]{1,0:T(8,128)(2,1)} %qup_hbm.1, ...), custom_call_target="tpu_custom_call" | custom-call | tf_op jit(solution)/shard_map/mla_up_backward/pallas_call | solution.py:358
  56.2 1.7 %write_results.1 = (f32[2,1536]{1,0:T(2,128)}, f32[2,512]{1,0:T(2,128)}, f32[96,384]{1,0:T(8,128)}, f32[32,512]{1,0:T(8,128)}) custom-call(f32[2,1536]{1,0:T(2,128)} %get-tuple-element.8.a, f32[2,512]{1,0:T(2,128)} %get-tuple-element.9.b, f32[96,384]{1,0:T(8,128)} %get-tuple-element.10.w, f32[32,512]{1,0:T(8,128)} %get-tuple-element.11.v), custom_call_target="tpu_custom_call" | custom-call | tf_op jit(solution)/shard_map/write_results/pallas_call | solution.py:386

commit v3 on v2

--- a/solution.py
+++ b/solution.py
@@ -30,12 +30,12 @@
 
 def kernel(
     ql_hbm, kvl_hbm, qg_hbm, kvg_hbm, qup_hbm, kvup_hbm, gq_hbm, gkv_hbm,
-    dql_hbm, dkvl_hbm, dqup_hbm, dkvup_hbm,
+    dql, dkvl, dqup, dkvup,
     ql, kvl, qg, kvg, qup, kvup, grads,
     pack, mixed, piece, gall, xall, part, near_in, send_far, far_in, natural, acc,
     load_sem, mix_send, mix_recv, plane_send, plane_recv, pair_send, pair_recv,
     rnear_send, rnear_recv, rfar_send, rfar_recv, afar_send, afar_recv, anear_send, anear_recv,
-    dql, dkvl, out_sem, ready,
+    ready,
 ):
     dp, tensor = lax.axis_index("dp"), lax.axis_index("tensor")
     c = lax.rem(dp, 2)
@@ -62,11 +62,11 @@
     peers += [along(dz, flip) for flip in (1, 0) for dz in (2, -2, 1, -1)]
     peers += [(lax.rem(dp + k, 16), tensor) for k in range(15, 0, -1)]
     peers += [along(0, 1)]
-    for peer in peers:
+    for peer in peers[:10]:
         pl.semaphore_signal(barrier, inc=1, device_id=peer, device_id_type=MESH)
 
     loads = [
-        pltpu.make_async_copy(src, dst, load_sem.at[n])
+        pltpu.make_async_copy(src, dst, load_sem.at[min(n, 4) if n < 6 else n - 1])
         for n, (src, dst) in enumerate([
             (ql_hbm, ql), (kvl_hbm, kvl), (qg_hbm, qg), (kvg_hbm, kvg),
             (gq_hbm, grads.at[:, 0:384]), (gkv_hbm, grads.at[:, 384:896]),
@@ -75,6 +75,8 @@
     ]
     for load in loads:
         load.start()
+    for peer in peers[10:]:
+        pl.semaphore_signal(barrier, inc=1, device_id=peer, device_id_type=MESH)
     sent = []
 
     def send(src, dst, send_sem, recv_sem, device):
@@ -84,6 +86,9 @@
         copy.start()
         return copy
 
+    def everything(at, sem):
+        return pltpu.make_async_copy(at, at, sem)
+
     with scope("w_loadsmall"):
         for load in loads[:4]:
             load.wait()
@@ -101,8 +106,7 @@
         pack[b, :, 96:128] = kv_normed[:, 32 * b : 32 * b + 32]
 
     with scope("w_loadgrads"):
-        for load in loads[4:6]:
-            load.wait()
+        everything(grads, load_sem.at[4]).wait()
     row, col = iota((128, 128), 0), iota((128, 128), 1)
     token = ((row >> 4) & 1) * 64 + ((row >> 1) & 7) * 8 + (row >> 5) * 2 + (row & 1)
     order = one_hot(col == token)
@@ -129,24 +133,24 @@
     mixes = []
     for k in range(1, 16):
         to = lax.rem(dp + k, 16)
-        mixes.append(send(pack.at[to], mixed.at[dp], mix_send.at[k], mix_recv.at[k], (to, tensor)))
+        mixes.append(send(pack.at[to], mixed.at[dp], mix_send.at[0], mix_recv.at[0], (to, tensor)))
 
     whole, low, high = pl.ds(0, 4), pl.ds(0, 2), pl.ds(2, 2)
 
     def pass_on(n, slot, dx, dy, rows=whole):
         at = gall.at[chip(*PLANE[n]), rows]
-        return send(at, at, plane_send.at[slot], plane_recv.at[slot], (chip(dx, dy), tensor))
+        return send(at, at, plane_send.at[0], plane_recv.at[slot - 1], (chip(dx, dy), tensor))
 
     def to_pair(n, slot, rows=whole):
         at = gall.at[chip(*PLANE[n]), rows]
-        return send(at, at, pair_send.at[slot], pair_recv.at[slot], (chip(0, 0, 1), tensor))
+        return send(at, at, pair_send.at[0], pair_recv.at[0], (chip(0, 0, 1), tensor))
 
     rnear = []
     for n, (s, flip) in enumerate(NEAR):
         device = along(steps[s], flip)
         half = 1 - xh if flip else xh
         cls = lax.rem(z + steps[s] + 32, 4)
-        rnear.append(send(part.at[cls, half], near_in.at[n], rnear_send.at[n], rnear_recv.at[n], device))
+        rnear.append(send(part.at[cls, half], near_in.at[n], rnear_send.at[0], rnear_recv.at[0], device))
 
     plane = {}
     plane[2] = pass_on(0, 2, 0, 1)
@@ -161,20 +165,19 @@
     pl.semaphore_signal(ready.at[3], inc=1, device_id=along(8), device_id_type=MESH)
 
     with scope("w_mixes"):
-        for copy in mixes:
-            copy.wait_recv()
+        everything(mixed.at[pl.ds(0, 15)], mix_recv.at[0]).wait()
     for b in range(16):
         piece[2 * b : 2 * b + 2, :] = mixed[b]
-    xall[xh, r, j] = piece[...].astype(BF16)
+    xall[xh * 4 + r, j] = piece[...].astype(BF16)
 
     def far_pass(k, slot, dz):
-        at = xall.at[xh, r, lax.rem(j + 8 - k, 8)]
-        return send(at, at, afar_send.at[slot], afar_recv.at[slot], along(dz))
+        at = xall.at[xh * 4 + r, lax.rem(j + 8 - k, 8)]
+        return send(at, at, afar_send.at[0], afar_recv.at[slot - 1], along(dz))
 
     def near_forward(k):
-        at = xall.at[xh, r, lax.rem(j + 8 - k, 8)]
+        at = xall.at[xh * 4 + r, lax.rem(j + 8 - k, 8)]
         for n, (s, flip) in enumerate(NEAR):
-            send(at, at, anear_send.at[n], anear_recv.at[n], along(steps[s], flip))
+            send(at, at, anear_send.at[0], anear_recv.at[0], along(steps[s], flip))
 
     afar = {}
     afar[2] = far_pass(0, 2, 8)
@@ -199,9 +202,8 @@
     await_plane(3)
     plane[8] = pass_on(3, 8, 0, 3, high)
     pairs.append(to_pair(3, 3))
-    for n, copy in enumerate(rnear):
-        with scope(f"w_rnear{n}"):
-            copy.wait_recv()
+    with scope("w_rnear"):
+        everything(near_in, rnear_recv.at[0]).wait()
     total = part[r, xh].astype(F32)
     for n in range(7):
         total = total + near_in[n].astype(F32)
@@ -217,20 +219,20 @@
 
     def far_sums(*slots):
         for k in slots:
-            rfar[k] = send(send_far.at[lax.rem(j + k, 8)], far_in.at[k], rfar_send.at[k], rfar_recv.at[k], along(4 * k))
-
-    far_sums(4, 3, 5)
+            rfar[k] = send(send_far.at[lax.rem(j + k, 8)], far_in.at[k], rfar_send.at[0], rfar_recv.at[0], along(4 * k))
+
+    far_sums(4)
     await_far(1)
     near_forward(1)
     await_far(7)
     near_forward(7)
     await_far(2)
-    afar[4] = far_pass(2, 4, 8)
+    await_far(6)
+    afar[4] = far_pass(2 + 4 * c, 4, 8 - 16 * c)
     afar[3] = far_pass(2, 3, 4)
+    afar[5] = far_pass(6, 5, -4)
+    far_sums(3, 5, 2, 6, 1, 7)
     near_forward(2)
-    await_far(6)
-    afar[5] = far_pass(6, 5, -4)
-    far_sums(2, 6, 1, 7)
     near_forward(6)
 
     await_plane(1)
@@ -260,22 +262,20 @@
     await_plane(9)
     pairs.append(to_pair(7, 8, high))
     with scope("w_pairs"):
-        for copy in pairs:
-            copy.wait_recv()
+        everything(gall.at[pl.ds(0, 8)], pair_recv.at[0]).wait()
 
     row, col = iota((256, 256), 0), iota((256, 256), 1)
     regroup = one_hot(col == ((row >> 1) & 15) * 16 + (row >> 5) * 2 + (row & 1))
 
     def weights(half, cls):
-        x = dot(xall[half, cls].reshape(256, 128), regroup, ((0,), (0,))).astype(BF16)
+        x = dot(xall[half * 4 + cls].reshape(256, 128), regroup, ((0,), (0,))).astype(BF16)
         g = gall[:, cls, half].reshape(256, 896)
         return dot(x, g, ((1,), (0,)))
 
     acc[...] = weights(xh, r)
 
-    for k in FAR:
-        with scope(f"w_rfar{k}"):
-            rfar[k].wait_recv()
+    with scope("w_rfar"):
+        everything(far_in.at[pl.ds(1, 7)], rfar_recv.at[0]).wait()
     latent = send_far[j].astype(F32)
     for k in range(1, 8):
         latent = latent + far_in[k].astype(F32)
@@ -293,56 +293,39 @@
     dql[...] = norm_back(natural[:, 0:1536], q_unit, q_inv, qg)
     dkvl[...] = norm_back(natural[:, 1536:2048], kv_unit, kv_inv, kvg)
 
-    outs = [
-        pltpu.make_async_copy(src, dst, out_sem.at[n])
-        for n, (src, dst) in enumerate([
-            (dql, dql_hbm), (dkvl, dkvl_hbm), (acc.at[0:96, 0:384], dqup_hbm), (acc.at[96:128, 384:896], dkvup_hbm)])
-    ]
-    outs[0].start()
-    outs[1].start()
-
-    def near_copy(n, at):
-        s, flip = NEAR[n]
-        return pltpu.make_async_remote_copy(
-            src_ref=at, dst_ref=at, send_sem=anear_send.at[n], recv_sem=anear_recv.at[n],
-            device_id=along(steps[s], flip), device_id_type=MESH)
-
     places = []
     for n, (s, flip) in enumerate(NEAR):
         half = 1 - xh if flip else xh
         cls = lax.rem(z - steps[s] + 32, 4)
         places.append((half, cls))
-        with scope(f"w_anear{n}"):
-            near_copy(n, xall.at[half, cls]).wait_recv()
+    with scope("w_anear"):
+        everything(xall.at[pl.ds(0, 7)], anear_recv.at[0]).wait()
     with scope("c_weights"):
         total = acc[...]
         for half, cls in places:
             total = total + weights(half, cls)
-        acc[...] = total
-    outs[2].start()
-    outs[3].start()
+        dqup[...] = total[0:96, 0:384]
+        dkvup[...] = total[96:128, 384:896]
 
     with scope("w_sends"):
-        for copy in mixes + list(plane.values()) + pairs + rnear + list(rfar.values()) + list(afar.values()):
-            copy.wait_send()
-        for n in range(7):
-            near_copy(n, xall.at[xh, r]).wait_send()
-    with scope("w_outs"):
-        for out in outs:
-            out.wait()
-
-
-def write_kernel(a, b, w, v, dql, dkvl, dqup, dkvup, at, bt, wt, vt, sem_in, sem_out):
-    stages = list(enumerate([(w, wt, dqup), (v, vt, dkvup), (a, at, dql), (b, bt, dkvl)]))
-    ins = [pltpu.make_async_copy(src, mid, sem_in.at[n]) for n, (src, mid, dst) in stages]
-    outs = [pltpu.make_async_copy(mid, dst, sem_out.at[n]) for n, (src, mid, dst) in stages]
-    for copy in ins:
+        everything(mixed.at[pl.ds(0, 15)], mix_send.at[0]).wait()
+        everything(gall.at[pl.ds(0, 7)], plane_send.at[0]).wait()
+        everything(gall.at[pl.ds(0, 8)], pair_send.at[0]).wait()
+        everything(near_in, rnear_send.at[0]).wait()
+        everything(far_in.at[pl.ds(1, 7)], rfar_send.at[0]).wait()
+        everything(xall.at[0, pl.ds(0, 7)], afar_send.at[0]).wait()
+        everything(xall.at[pl.ds(0, 7)], anear_send.at[0]).wait()
+
+
+def write_kernel(a, b, w, v, dql, dkvl, dqup, dkvup, sem):
+    copies = [
+        pltpu.make_async_copy(src, dst, sem.at[n])
+        for n, (src, dst) in enumerate([(w, dqup), (v, dkvup), (a, dql), (b, dkvl)])
+    ]
+    for copy in copies:
         copy.start()
-    for copy, out in zip(ins, outs):
+    for copy in copies:
         copy.wait()
-        out.start()
-    for out in outs:
-        out.wait()
 
 
 def body(query_latent, key_value_latent, query_gain, key_value_gain, q_up, kv_up, grad_q, grad_kv):
@@ -358,9 +341,9 @@
     results = pl.pallas_call(
         kernel,
         name="mla_up_backward",
-        out_shape=shapes,
+        out_shape=tuple(vmem(shape.shape, F32) for shape in shapes),
         in_specs=[hbm] * 8,
-        out_specs=(hbm,) * 4,
+        out_specs=(pl.BlockSpec(memory_space=pltpu.VMEM),) * 4,
         scratch_shapes=[
             vmem((2, 1536), BF16), vmem((2, 512), BF16), vmem((1536,), F32), vmem((512,), F32),
             vmem((1536, 384), BF16), vmem((512, 512), BF16), vmem((128, 896), BF16),
@@ -368,29 +351,28 @@
             vmem((16, 2, 128), F32),
             vmem((32, 128), F32),
             vmem((16, 4, 2, 16, 896), BF16),
-            vmem((2, 4, 8, 32, 128), BF16),
+            vmem((8, 8, 32, 128), BF16),
             vmem((4, 2, 4, 16, 512), BF16),
             vmem((7, 4, 16, 512), BF16),
             vmem((8, 8, 512), BF16),
             vmem((8, 8, 512), BF16),
             vmem((2, 2048), F32),
             vmem((128, 896), F32),
-            dma((8,)), dma((16,)), dma((16,)), dma((10,)), dma((10,)), dma((9,)), dma((9,)),
-            dma((7,)), dma((7,)), dma((8,)), dma((8,)), dma((8,)), dma((8,)), dma((7,)), dma((7,)),
-            vmem((2, 1536), F32), vmem((2, 512), F32), dma((4,)),
+            dma((7,)), dma((1,)), dma((1,)), dma((1,)), dma((9,)), dma((1,)), dma((1,)),
+            dma((1,)), dma((1,)), dma((1,)), dma((1,)), dma((1,)), dma((7,)), dma((1,)), dma((1,)),
             pltpu.SemaphoreType.REGULAR((4,)),
         ],
         compiler_params=pltpu.CompilerParams(
-            collective_id=0, has_side_effects=True, vmem_limit_bytes=67043328),
+            collective_id=0, has_side_effects=True, vmem_limit_bytes=60 * 1000 * 1000),
     )(query_latent, key_value_latent, query_gain, key_value_gain, q_up, kv_up, grad_q, grad_kv)
     return pl.pallas_call(
         write_kernel,
         name="write_results",
         out_shape=shapes,
-        in_specs=[hbm] * 4,
+        in_specs=[pl.BlockSpec(memory_space=pltpu.VMEM)] * 4,
         out_specs=(hbm,) * 4,
-        scratch_shapes=[vmem(shape.shape, F32) for shape in shapes] + [dma((4,)), dma((4,))],
-        compiler_params=pltpu.CompilerParams(vmem_limit_bytes=67043328),
+        scratch_shapes=[dma((4,))],
+        compiler_params=pltpu.CompilerParams(vmem_limit_bytes=1024 * 1024),
     )(*results)
 
 

time: 58.1 us -> 54.1 us (0.931)
  Pallas kernels: 57.2 us -> 53.3 us
    pallas_call x1, Pallas kernels: 55.6 us -> 52.6 us  [body(): pl.pallas_call(kernel, name='mla_up_backward', out_shape=tuple((vmem(shap...]
    pallas_call x1, Pallas kernels: 1.66 us -> 0.72 us  [body(): pl.pallas_call(write_kernel, name='write_results', out_shape=shapes, in_s...]
where the time goes in v3:
time: 54.1 us; the launch traced here: 54 us
  Pallas kernels  53.3 us (99%)
  between operations  0.64 us (1%)
    pallas_call x1, Pallas kernels, body(): pl.pallas_call(kernel, name='mla_up_backward', out_shape=tuple((vmem(shap...  52.6 us

profile of v3, /device:TPU:1, one launch (start us, length us, event | category | flops | bytes accessed | tf_op | source)
XLA Modules:
  0.0 54.0 jit_solution(14695058652219407265)
XLA Ops:
  0.6 52.6 %mla_up_backward.1 = (f32[2,1536]{1,0:T(2,128)S(1)}, f32[2,512]{1,0:T(2,128)S(1)}, f32[96,384]{1,0:T(8,128)S(1)}, f32[32,512]{1,0:T(8,128)S(1)}) custom-call(bf16[2,1536]{1,0:T(2,128)(2,1)} %ql_hbm.1, bf16[2,512]{1,0:T(2,128)(2,1)} %kvl_hbm.1, f32[1536]{0:T(1024)} %qg_hbm.1, f32[512]{0:T(512)} %kvg_hbm.1, bf16[1536,384]{1,0:T(8,128)(2,1)} %qup_hbm.1, ...), custom_call_target="tpu_custom_call" | custom-call | tf_op jit(solution)/shard_map/mla_up_backward/pallas_call | solution.py:341
  53.2 0.7 %write_results.1 = (f32[2,1536]{1,0:T(2,128)}, f32[2,512]{1,0:T(2,128)}, f32[96,384]{1,0:T(8,128)}, f32[32,512]{1,0:T(8,128)}) custom-call(f32[2,1536]{1,0:T(2,128)S(1)} %get-tuple-element.8.a, f32[2,512]{1,0:T(2,128)S(1)} %get-tuple-element.9.b, f32[96,384]{1,0:T(8,128)S(1)} %get-tuple-element.10.w, f32[32,512]{1,0:T(8,128)S(1)} %get-tuple-element.11.v), custom_call_target="tpu_custom_call" | custom-call | tf_op jit(solution)/shard_map/write_results/pallas_call | solution.py:368

commit v4 on v3

--- a/solution.py
+++ b/solution.py
@@ -32,7 +32,7 @@
     ql_hbm, kvl_hbm, qg_hbm, kvg_hbm, qup_hbm, kvup_hbm, gq_hbm, gkv_hbm,
     dql, dkvl, dqup, dkvup,
     ql, kvl, qg, kvg, qup, kvup, grads,
-    pack, mixed, piece, gall, xall, part, near_in, send_far, far_in, natural, acc,
+    pack, mixed, piece, gall, xall, xlate, glate, part, near_in, send_far, far_in, natural, acc,
     load_sem, mix_send, mix_recv, plane_send, plane_recv, pair_send, pair_recv,
     rnear_send, rnear_recv, rfar_send, rfar_recv, afar_send, afar_recv, anear_send, anear_recv,
     ready,
@@ -125,6 +125,15 @@
             value = dot(own[:, 384:896], kvup[...], ((1,), (1,)))
         part[:, :, q] = value.astype(BF16).reshape(4, 2, 16, 512)
 
+    classes = []
+    for s, flip in [(0, 0)] + NEAR:
+        at = lax.rem(z - steps[s] + 32, 32)
+        late = [lax.rem(at // 4 + 8 - k, 8) for k in (3, 4, 5)]
+        classes.append((1 - xh if flip else xh, lax.rem(at, 4), late))
+    for half, cls, late in classes:
+        for place in late:
+            xall[half * 4 + cls, place] = jnp.zeros((32, 128), BF16)
+
     with scope("w_barrier"):
         pl.semaphore_wait(barrier, len(peers))
     pl.semaphore_signal(ready.at[0], inc=1, device_id=along(-4), device_id_type=MESH)
@@ -170,14 +179,18 @@
         piece[2 * b : 2 * b + 2, :] = mixed[b]
     xall[xh * 4 + r, j] = piece[...].astype(BF16)
 
+    mine = xh * 4 + r
+
     def far_pass(k, slot, dz):
-        at = xall.at[xh * 4 + r, lax.rem(j + 8 - k, 8)]
-        return send(at, at, afar_send.at[0], afar_recv.at[slot - 1], along(dz))
+        at = xall.at[mine, lax.rem(j + 8 - k, 8)]
+        to = xlate.at[slot - 3, mine] if slot in (3, 4, 5) else at
+        return send(at, to, afar_send.at[0], afar_recv.at[slot - 1], along(dz))
 
     def near_forward(k):
-        at = xall.at[xh * 4 + r, lax.rem(j + 8 - k, 8)]
-        for n, (s, flip) in enumerate(NEAR):
-            send(at, at, anear_send.at[0], anear_recv.at[0], along(steps[s], flip))
+        late = 1 if k in (3, 4, 5) else 0
+        at = xlate.at[k - 3, mine] if late else xall.at[mine, lax.rem(j + 8 - k, 8)]
+        for s, flip in NEAR:
+            send(at, at, anear_send.at[late], anear_recv.at[late], along(steps[s], flip))
 
     afar = {}
     afar[2] = far_pass(0, 2, 8)
@@ -250,13 +263,13 @@
     near_forward(3)
     await_far(5)
     near_forward(5)
+    await_far(4)
+    near_forward(4)
 
     await_plane(4)
     pairs.append(to_pair(4, 4))
     await_plane(5)
     pairs.append(to_pair(5, 5))
-    await_far(4)
-    near_forward(4)
     await_plane(7)
     pairs.append(to_pair(7, 7, low))
     await_plane(9)
@@ -273,6 +286,19 @@
         return dot(x, g, ((1,), (0,)))
 
     acc[...] = weights(xh, r)
+    row, col = iota((32, 256), 0), iota((32, 256), 1)
+    for half, cls, late in classes:
+        for n, place in enumerate(late):
+            pick = one_hot(col == (row >> 1) * 16 + 2 * place + (row & 1))
+            glate[n, half * 4 + cls] = dot(pick, gall[:, cls, half].reshape(256, 896), ((1,), (0,))).astype(BF16)
+
+    with scope("w_anear"):
+        everything(xall.at[pl.ds(0, 7), pl.ds(0, 5)], anear_recv.at[0]).wait()
+    with scope("c_weights"):
+        total = acc[...]
+        for half, cls, late in classes[1:]:
+            total = total + weights(half, cls)
+        acc[...] = total
 
     with scope("w_rfar"):
         everything(far_in.at[pl.ds(1, 7)], rfar_recv.at[0]).wait()
@@ -293,17 +319,12 @@
     dql[...] = norm_back(natural[:, 0:1536], q_unit, q_inv, qg)
     dkvl[...] = norm_back(natural[:, 1536:2048], kv_unit, kv_inv, kvg)
 
-    places = []
-    for n, (s, flip) in enumerate(NEAR):
-        half = 1 - xh if flip else xh
-        cls = lax.rem(z - steps[s] + 32, 4)
-        places.append((half, cls))
-    with scope("w_anear"):
-        everything(xall.at[pl.ds(0, 7)], anear_recv.at[0]).wait()
-    with scope("c_weights"):
+    with scope("w_late"):
+        everything(xlate.at[:, pl.ds(0, 7)], anear_recv.at[1]).wait()
+    with scope("c_late"):
         total = acc[...]
-        for half, cls in places:
-            total = total + weights(half, cls)
+        for n in range(3):
+            total = total + dot(xlate[n].reshape(256, 128), glate[n].reshape(256, 896), ((0,), (0,)))
         dqup[...] = total[0:96, 0:384]
         dkvup[...] = total[96:128, 384:896]
 
@@ -314,7 +335,8 @@
         everything(near_in, rnear_send.at[0]).wait()
         everything(far_in.at[pl.ds(1, 7)], rfar_send.at[0]).wait()
         everything(xall.at[0, pl.ds(0, 7)], afar_send.at[0]).wait()
-        everything(xall.at[pl.ds(0, 7)], anear_send.at[0]).wait()
+        everything(xall.at[pl.ds(0, 7), pl.ds(0, 5)], anear_send.at[0]).wait()
+        everything(xlate.at[:, pl.ds(0, 7)], anear_send.at[1]).wait()
 
 
 def write_kernel(a, b, w, v, dql, dkvl, dqup, dkvup, sem):
@@ -352,6 +374,8 @@
             vmem((32, 128), F32),
             vmem((16, 4, 2, 16, 896), BF16),
             vmem((8, 8, 32, 128), BF16),
+            vmem((3, 8, 32, 128), BF16),
+            vmem((3, 8, 32, 896), BF16),
             vmem((4, 2, 4, 16, 512), BF16),
             vmem((7, 4, 16, 512), BF16),
             vmem((8, 8, 512), BF16),
@@ -359,7 +383,7 @@
             vmem((2, 2048), F32),
             vmem((128, 896), F32),
             dma((7,)), dma((1,)), dma((1,)), dma((1,)), dma((9,)), dma((1,)), dma((1,)),
-            dma((1,)), dma((1,)), dma((1,)), dma((1,)), dma((1,)), dma((7,)), dma((1,)), dma((1,)),
+            dma((1,)), dma((1,)), dma((1,)), dma((1,)), dma((1,)), dma((7,)), dma((2,)), dma((2,)),
             pltpu.SemaphoreType.REGULAR((4,)),
         ],
         compiler_params=pltpu.CompilerParams(

time: 54.1 us -> 52.9 us (0.978)
  Pallas kernels: 53.3 us -> 52.1 us
    pallas_call x1, Pallas kernels: 52.6 us -> 51.4 us  [body(): pl.pallas_call(kernel, name='mla_up_backward', out_shape=tuple((vmem(shap...]
where the time goes in v4:
time: 52.9 us; the launch traced here: 52.7 us
  Pallas kernels  52.1 us (98%)
  between operations  0.64 us (1%)
    pallas_call x1, Pallas kernels, body(): pl.pallas_call(kernel, name='mla_up_backward', out_shape=tuple((vmem(shap...  51.4 us

profile of v4, /device:TPU:1, one launch (start us, length us, event | category | flops | bytes accessed | tf_op | source)
XLA Modules:
  0.0 52.7 jit_solution(1274319070900392754)
XLA Ops:
  0.6 51.4 %mla_up_backward.1 = (f32[2,1536]{1,0:T(2,128)S(1)}, f32[2,512]{1,0:T(2,128)S(1)}, f32[96,384]{1,0:T(8,128)S(1)}, f32[32,512]{1,0:T(8,128)S(1)}) custom-call(bf16[2,1536]{1,0:T(2,128)(2,1)} %ql_hbm.1, bf16[2,512]{1,0:T(2,128)(2,1)} %kvl_hbm.1, f32[1536]{0:T(1024)} %qg_hbm.1, f32[512]{0:T(512)} %kvg_hbm.1, bf16[1536,384]{1,0:T(8,128)(2,1)} %qup_hbm.1, ...), custom_call_target="tpu_custom_call" | custom-call | tf_op jit(solution)/shard_map/mla_up_backward/pallas_call | solution.py:363
  52.0 0.7 %write_results.1 = (f32[2,1536]{1,0:T(2,128)}, f32[2,512]{1,0:T(2,128)}, f32[96,384]{1,0:T(8,128)}, f32[32,512]{1,0:T(8,128)}) custom-call(f32[2,1536]{1,0:T(2,128)S(1)} %get-tuple-element.8.a, f32[2,512]{1,0:T(2,128)S(1)} %get-tuple-element.9.b, f32[96,384]{1,0:T(8,128)S(1)} %get-tuple-element.10.w, f32[32,512]{1,0:T(8,128)S(1)} %get-tuple-element.11.v), custom_call_target="tpu_custom_call" | custom-call | tf_op jit(solution)/shard_map/write_results/pallas_call | solution.py:392

commit v5 on v4

--- a/solution.py
+++ b/solution.py
@@ -288,9 +288,9 @@
     acc[...] = weights(xh, r)
     row, col = iota((32, 256), 0), iota((32, 256), 1)
     for half, cls, late in classes:
-        for n, place in enumerate(late):
-            pick = one_hot(col == (row >> 1) * 16 + 2 * place + (row & 1))
-            glate[n, half * 4 + cls] = dot(pick, gall[:, cls, half].reshape(256, 896), ((1,), (0,))).astype(BF16)
+        pick = jnp.concatenate([one_hot(col == (row >> 1) * 16 + 2 * place + (row & 1)) for place in late], axis=0)
+        rows = dot(pick, gall[:, cls, half].reshape(256, 896), ((1,), (0,))).astype(BF16)
+        glate[:, half * 4 + cls] = rows.reshape(3, 32, 896)
 
     with scope("w_anear"):
         everything(xall.at[pl.ds(0, 7), pl.ds(0, 5)], anear_recv.at[0]).wait()

time: 52.9 us -> 52.9 us (level)
  no operation moved by 1% of the time
where the time goes in v5:
time: 52.9 us; the launch traced here: 52.7 us
  Pallas kernels  52.1 us (98%)
  between operations  0.64 us (1%)
    pallas_call x1, Pallas kernels, body(): pl.pallas_call(kernel, name='mla_up_backward', out_shape=tuple((vmem(shap...  51.4 us

profile of v5, /device:TPU:1, one launch (start us, length us, event | category | flops | bytes accessed | tf_op | source)
XLA Modules:
  0.0 52.7 jit_solution(16677545074863828714)
XLA Ops:
  0.6 51.4 %mla_up_backward.1 = (f32[2,1536]{1,0:T(2,128)S(1)}, f32[2,512]{1,0:T(2,128)S(1)}, f32[96,384]{1,0:T(8,128)S(1)}, f32[32,512]{1,0:T(8,128)S(1)}) custom-call(bf16[2,1536]{1,0:T(2,128)(2,1)} %ql_hbm.1, bf16[2,512]{1,0:T(2,128)(2,1)} %kvl_hbm.1, f32[1536]{0:T(1024)} %qg_hbm.1, f32[512]{0:T(512)} %kvg_hbm.1, bf16[1536,384]{1,0:T(8,128)(2,1)} %qup_hbm.1, ...), custom_call_target="tpu_custom_call" | custom-call | tf_op jit(solution)/shard_map/mla_up_backward/pallas_call | solution.py:363
  52.0 0.7 %write_results.1 = (f32[2,1536]{1,0:T(2,128)}, f32[2,512]{1,0:T(2,128)}, f32[96,384]{1,0:T(8,128)}, f32[32,512]{1,0:T(8,128)}) custom-call(f32[2,1536]{1,0:T(2,128)S(1)} %get-tuple-element.8.a, f32[2,512]{1,0:T(2,128)S(1)} %get-tuple-element.9.b, f32[96,384]{1,0:T(8,128)S(1)} %get-tuple-element.10.w, f32[32,512]{1,0:T(8,128)S(1)} %get-tuple-element.11.v), custom_call_target="tpu_custom_call" | custom-call | tf_op jit(solution)/shard_map/write_results/pallas_call | solution.py:392
